TPU v7x, 32 devices: a whole 2x2x4 slice. The times are simulated.
32 devices in a mesh: grp: 8 (over y, x, core), shard: 4 (over z).
Axes of the slice: x: 2, y: 2, z: 4, core: 2. Of those that a mesh axis runs over, the one named last changes fastest.
Arguments:
- gradients: bfloat16 [8, 1024, 5120], P('grp', None, 'shard'), may hold values from -150 to 150
- left_factor: bfloat16 [8, 1024, 1024], P('grp'), may hold values from -1 to 2, as said below
- right_factor: bfloat16 [8, 5120, 5120], P('grp', 'shard'), may hold values from -1 to 2, as said below
Outputs:
- update: bfloat16 [8, 1024, 5120], P('grp', None, 'shard')
Inputs may be any that keep to these rules, and one draw needn't show every extreme that they name: `left_factor`: each factor is upper triangular with a positive diagonal. `right_factor`: each factor is upper triangular with a positive diagonal.
All inputs are finite; a program needn't handle non-finite values.
Results may differ from a plain program's by a relative error of at most 0.0061.
Values may be sent and summed in bfloat16 or wider, within the bound.
A program may use at most 128 MiB of HBM per device.

v0:
```python
import jax
import jax.numpy as jnp
from jax import lax
from jax.sharding import PartitionSpec as P


def body(gradients, left_factor, right_factor):
    squares = jnp.float32(0.0)
    gradient = gradients[0]
    left_q = left_factor[0]
    right_rows = right_factor[0]
    block = right_rows
    first = lax.dot_general(
        lax.all_gather(gradient, "shard", axis=1, tiled=True),
        block,
        (((1,), (1,)), ((), ())),
        preferred_element_type=jnp.float32,
    ).astype(jnp.bfloat16)
    block = right_rows
    second_rows = lax.psum_scatter(
        lax.dot_general(block, first, (((0,), (1,)), ((), ())), preferred_element_type=jnp.float32),
        "shard",
        scatter_dimension=0,
        tiled=True,
    ).astype(jnp.bfloat16)
    second = second_rows.T
    third = jnp.dot(left_q, second, preferred_element_type=jnp.float32).astype(jnp.bfloat16)
    precond = lax.dot_general(
        left_q, third, (((0,), (0,)), ((), ())), preferred_element_type=jnp.float32
    )
    results = [precond]
    squares = jnp.sum(precond * precond)
    total = lax.psum(squares, ("grp", "shard"))
    count = (
        gradients.shape[0]
        * lax.axis_size("grp")
        * gradients.shape[1]
        * gradients.shape[2]
        * lax.axis_size("shard")
    )
    rms = jnp.sqrt(total / count + 1e-06)
    factor = jnp.minimum(jnp.float32(1.0), 1.1 / rms)
    stacked = jnp.stack(results, axis=0)
    return (stacked * factor).astype(jnp.bfloat16)


def solution(mesh):
    in_specs = (P("grp", None, "shard"), P("grp", None, None), P("grp", "shard", None))
    out_specs = P("grp", None, "shard")
    return jax.shard_map(body, mesh=mesh, in_specs=in_specs, out_specs=out_specs, check_vma=False)
```

profile of v0, /device:TPU:0, one launch (start us, length us, event | category | flops | bytes accessed | tf_op | source)
XLA Modules:
  0.0 647.6 jit_solution(3090217392802980609)
XLA Ops:
  6.5 0.0 copy-start
  6.5 0.0 all-gather.3.cloned.1.call-start
  6.5 0.7 all-gather.3.cloned.1.call-update
  7.3 0.0 reduce-scatter.2.cloned.1.call-start
  7.3 188.3 %all-gather.3.cloned.1.call-done = bf16[1,1024,5120]{2,1,0:T(8,128)(2,1)} async-done(((bf16[1,1024,1280]{2,1,0:T(8,128)(2,1)}), bf16[1,1024,5120]{2,1,0:T(8,128)(2,1)}) %all-gather.3.cloned.1.call-update) | async-done | bytes 10485776 | tf_op jit(solution)/shard_map/all_gather | solution.py:14
  195.6 17.5 %fusion.8 = bf16[1024,1280]{1,0:T(8,128)(2,1)S(1)} fusion(bf16[1,1280,5120]{2,1,0:T(8,128)(2,1)} %param.5, bf16[1,1024,5120]{2,1,0:T(8,128)(2,1)} %all-gather.3.cloned.1.call-done), kind=kOutput, calls=%fused_computation.8 | convolution fusion | flops 13423083520 | bytes 26214400 | tf_op jit(solution)/shard_map/dot_general | solution.py:13
  213.0 20.6 %fusion.4 = f32[5120,1024]{0,1:T(8,128)} fusion(bf16[1024,1280]{1,0:T(8,128)(2,1)S(1)} %fusion.8, bf16[1,1280,5120]{2,1,0:T(8,128)(2,1)} %param.5), kind=kOutput, calls=%fused_computation.4 | convolution fusion | flops 13421772800 | bytes 36700160 | tf_op jit(solution)/shard_map/dot_general | solution.py:21
  233.6 0.0 reduce-scatter.2.cloned.1.call-update
  233.7 345.7 %reduce-scatter.2.cloned.1.call-done = f32[1280,1024]{0,1:T(8,128)} async-done(((f32[5120,1024]{0,1:T(8,128)}), f32[1280,1024]{0,1:T(8,128)}) %reduce-scatter.2.cloned.1.call-update) | async-done | bytes 5242896 | tf_op jit(solution)/shard_map/reduce_scatter | solution.py:20
  579.4 0.0 copy-done
  579.4 9.9 %multiply_reduce_fusion = (f32[]{:T(128)}, f32[1280,1024]{1,0:T(8,128)}) fusion(bf16[1,1024,1024]{2,1,0:T(8,128)(2,1)S(1)} %copy-done, f32[1280,1024]{0,1:T(8,128)} %reduce-scatter.2.cloned.1.call-done), kind=kOutput, calls=%fused_computation.7 | convolution fusion | flops 5373952000 | bytes 12582916 | tf_op jit(solution)/shard_map/dot_general | solution.py:28
  589.3 41.7 %psum.7 = f32[]{:T(128)} all-reduce(f32[]{:T(128)} %get-tuple-element.5), channel_id=1, replica_groups=mesh['grp'=8,'shard'=4] {'grp','shard'}, use_global_device_ids=true, to_apply=%region_2.0 | all-reduce | flops 1 | bytes 8 | tf_op jit(solution)/shard_map/psum | solution.py:33
  631.7 4.7 fusion.13
  636.4 4.4 copy.4
Async XLA Ops:
  6.5 572.8 %copy-start = (bf16[1,1024,1024]{2,1,0:T(8,128)(2,1)S(1)}, bf16[1,1024,1024]{2,1,0:T(8,128)(2,1)}, u32[]{:S(2)}) copy-start(bf16[1,1024,1024]{2,1,0:T(8,128)(2,1)} %param.4) | copy-start | bytes 6291460
  6.5 189.0 %all-gather.3.cloned.1.call-start = ((), (), s32[]{:S(2)}) async-start(), calls=%async_computation.2 | async-start | bytes 13107200 | tf_op jit(solution)/shard_map/all_gather | solution.py:14
  7.3 572.1 %reduce-scatter.2.cloned.1.call-start = ((), (), s32[]{:S(2)}) async-start(), calls=%async_computation.1 | async-start | bytes 26214400 | tf_op jit(solution)/shard_map/reduce_scatter | solution.py:20
Sparse Core Ops, SparseCore 0:
  8.9 186.6 all-gather.2
  233.8 345.5 reduce-scatter.1
where the time goes:
time: 648 us
  waiting for transfers between devices  535 us (83%)
  matrix products  48 us (7%)
  blocking collectives  41.7 us (6%)
  between operations  14.1 us (2%)
    reduce_scatter x1, waiting for transfers between devices, body(): lax.psum_scatter(lax.dot_general(block, first, (((0,), (1,)), ((), ())),...  346 us
    all_gather x1, waiting for transfers between devices, body(): lax.all_gather(gradient, 'shard', axis=1, tiled=True)  188 us
    psum x1, blocking collectives, body(): total = lax.psum(squares, ('grp', 'shard'))  41.7 us
    dot_general x1, matrix products, body(): lax.dot_general(block, first, (((0,), (1,)), ((), ())), preferred_element...  20.6 us
    dot_general x1, matrix products, body(): lax.dot_general(lax.all_gather(gradient, 'shard', axis=1, tiled=True), bl...  17.5 us
  transfers between devices with their start and end apart: 2, of which 2 were waited for; matrix products, arithmetic and copies ran while one was open for 0% of the time, Pallas kernels for 0%

commit v1 on v0

--- a/solution.py
+++ b/solution.py
@@ -30,7 +30,7 @@
     )
     results = [precond]
     squares = jnp.sum(precond * precond)
-    total = lax.psum(squares, ("grp", "shard"))
+    total = lax.psum(lax.psum(squares, "grp"), "shard")
     count = (
         gradients.shape[0]
         * lax.axis_size("grp")

time: 648 us -> 633 us (0.977)
  blocking collectives: 41.7 us -> 26.7 us
    psum x1 -> x2, blocking collectives: 41.7 us -> 26.7 us  [body(): total = lax.psum(lax.psum(squares, 'grp'), 'shard')]
where the time goes in v1:
time: 633 us
  waiting for transfers between devices  535 us (85%)
  matrix products  48 us (8%)
  blocking collectives  26.7 us (4%)
  between operations  14.1 us (2%)
    reduce_scatter x1, waiting for transfers between devices, body(): lax.psum_scatter(lax.dot_general(block, first, (((0,), (1,)), ((), ())),...  346 us
    all_gather x1, waiting for transfers between devices, body(): lax.all_gather(gradient, 'shard', axis=1, tiled=True)  188 us
    psum x2, blocking collectives, body(): total = lax.psum(lax.psum(squares, 'grp'), 'shard')  26.7 us
    dot_general x1, matrix products, body(): lax.dot_general(block, first, (((0,), (1,)), ((), ())), preferred_element...  20.6 us
    dot_general x1, matrix products, body(): lax.dot_general(lax.all_gather(gradient, 'shard', axis=1, tiled=True), bl...  17.5 us
  transfers between devices with their start and end apart: 2, of which 2 were waited for; matrix products, arithmetic and copies ran while one was open for 0% of the time, Pallas kernels for 0%

profile of v1, /device:TPU:0, one launch (start us, length us, event | category | flops | bytes accessed | tf_op | source)
XLA Modules:
  0.0 632.7 jit_solution(1848564641300166080)
XLA Ops:
  6.5 0.0 copy-start
  6.5 0.0 all-gather.3.cloned.1.call-start
  6.5 0.7 all-gather.3.cloned.1.call-update
  7.3 0.0 reduce-scatter.2.cloned.1.call-start
  7.3 188.3 %all-gather.3.cloned.1.call-done = bf16[1,1024,5120]{2,1,0:T(8,128)(2,1)} async-done(((bf16[1,1024,1280]{2,1,0:T(8,128)(2,1)}), bf16[1,1024,5120]{2,1,0:T(8,128)(2,1)}) %all-gather.3.cloned.1.call-update) | async-done | bytes 10485776 | tf_op jit(solution)/shard_map/all_gather | solution.py:14
  195.6 17.5 %fusion.8 = bf16[1024,1280]{1,0:T(8,128)(2,1)S(1)} fusion(bf16[1,1280,5120]{2,1,0:T(8,128)(2,1)} %param.5, bf16[1,1024,5120]{2,1,0:T(8,128)(2,1)} %all-gather.3.cloned.1.call-done), kind=kOutput, calls=%fused_computation.8 | convolution fusion | flops 13423083520 | bytes 26214400 | tf_op jit(solution)/shard_map/dot_general | solution.py:13
  213.0 20.6 %fusion.4 = f32[5120,1024]{0,1:T(8,128)} fusion(bf16[1024,1280]{1,0:T(8,128)(2,1)S(1)} %fusion.8, bf16[1,1280,5120]{2,1,0:T(8,128)(2,1)} %param.5), kind=kOutput, calls=%fused_computation.4 | convolution fusion | flops 13421772800 | bytes 36700160 | tf_op jit(solution)/shard_map/dot_general | solution.py:21
  233.6 0.0 reduce-scatter.2.cloned.1.call-update
  233.7 345.7 %reduce-scatter.2.cloned.1.call-done = f32[1280,1024]{0,1:T(8,128)} async-done(((f32[5120,1024]{0,1:T(8,128)}), f32[1280,1024]{0,1:T(8,128)}) %reduce-scatter.2.cloned.1.call-update) | async-done | bytes 5242896 | tf_op jit(solution)/shard_map/reduce_scatter | solution.py:20
  579.4 0.0 copy-done
  579.4 9.9 %multiply_reduce_fusion = (f32[]{:T(128)}, f32[1280,1024]{1,0:T(8,128)}) fusion(bf16[1,1024,1024]{2,1,0:T(8,128)(2,1)S(1)} %copy-done, f32[1280,1024]{0,1:T(8,128)} %reduce-scatter.2.cloned.1.call-done), kind=kOutput, calls=%fused_computation.7 | convolution fusion | flops 5373952000 | bytes 12582916 | tf_op jit(solution)/shard_map/dot_general | solution.py:28
  589.3 13.8 %psum.14 = f32[]{:T(128)} all-reduce(f32[]{:T(128)} %get-tuple-element.5), channel_id=1, replica_groups=mesh['grp'=8,'shard'=4] {'grp'}, use_global_device_ids=true, to_apply=%region_2.0 | all-reduce | flops 1 | bytes 8 | tf_op jit(solution)/shard_map/psum | solution.py:33
  603.1 12.9 %psum.15 = f32[]{:T(128)} all-reduce(f32[]{:T(128)} %psum.14), channel_id=1, replica_groups=mesh['grp'=8,'shard'=4] {'shard'}, use_global_device_ids=true, to_apply=%region_3.0 | all-reduce | flops 1 | bytes 8 | tf_op jit(solution)/shard_map/psum | solution.py:33
  616.7 4.7 fusion.13
  621.5 4.4 copy.4
Async XLA Ops:
  6.5 572.8 %copy-start = (bf16[1,1024,1024]{2,1,0:T(8,128)(2,1)S(1)}, bf16[1,1024,1024]{2,1,0:T(8,128)(2,1)}, u32[]{:S(2)}) copy-start(bf16[1,1024,1024]{2,1,0:T(8,128)(2,1)} %param.4) | copy-start | bytes 6291460
  6.5 189.0 %all-gather.3.cloned.1.call-start = ((), (), s32[]{:S(2)}) async-start(), calls=%async_computation.2 | async-start | bytes 13107200 | tf_op jit(solution)/shard_map/all_gather | solution.py:14
  7.3 572.1 %reduce-scatter.2.cloned.1.call-start = ((), (), s32[]{:S(2)}) async-start(), calls=%async_computation.1 | async-start | bytes 26214400 | tf_op jit(solution)/shard_map/reduce_scatter | solution.py:20
Sparse Core Ops, SparseCore 0:
  8.9 186.6 all-gather.2
  233.8 345.5 reduce-scatter.1
